TPU v7x, 32 devices: a whole 2x2x4 slice. The times are simulated.
32 devices in a mesh: grp: 2 (over y), tgt: 4 (over z), src: 4 (over x, core).
Axes of the slice: x: 2, y: 2, z: 4, core: 2. Of those that a mesh axis runs over, the one named last changes fastest.
Arguments:
- target_rows: bfloat16 [2048, 4608], P(('grp', 'tgt', 'src')), parts along dimension 0, may hold values from -6 to 6
- target_pos: int32 [2048], P(('grp', 'tgt')), parts along dimension 0, may hold values from 0 to 255
- decoder_rows: bfloat16 [512, 4608], P(('grp', 'tgt', 'src')), parts along dimension 0, may hold values from -0.09375 to 0.09375
- source_pos: int32 [512], P('grp'), parts along dimension 0, may hold values from 0 to 255
- out_proj: bfloat16 [32, 4608, 128], P('src', 'tgt'), may hold values from -0.09375 to 0.09375
- value_proj: bfloat16 [16, 4608, 128], P('src'), may hold values from -1 to 1
- attention: bfloat16 [64, 256, 256], P(('grp', 'src'), 'tgt'), parts along dimension 0, may hold values from 0 to 1, as said below
- tile_pattern: int32 [8, 4], P('grp'), parts along dimension 0, may hold values from 0 to 1, as said below
Outputs:
- edges: bfloat16 [512, 1024], P(('grp', 'src'), 'tgt'), parts along dimension 0
There are 2 independent parts, one for each index of `grp`. A program takes and returns all parts, laid end to end along the dimension named above; an argument that names none is the same for every part. Nothing has to cross between parts.
Inputs may be any that keep to these rules, and one draw needn't show every extreme that they name: Each row attention[h, p, :] is a probability distribution over the keys 0 to p: zero beyond p, summing to one. tile_pattern[b, c] is 1 where the tile of edges between source block b and target block c is kept, else 0.
All inputs are finite; a program needn't handle non-finite values.
Results may differ from a plain program's by a relative error of at most 0.0057.
Values may be sent and summed in bfloat16 or wider, within the bound.
A program may use at most 64 MiB of HBM per device.

v0:
```python
import jax
import jax.numpy as jnp
from jax import lax
from jax.sharding import PartitionSpec as P


def passed_along(value, axis, steps):
    count = lax.axis_size(axis)
    pairs = [(source, (source + steps) % count) for source in range(count)]
    return lax.ppermute(value, axis, pairs)


def shards(
    target_rows, target_pos, decoder_rows, source_pos, out_proj, value_proj, attention, tile_pattern
):
    blocks = lax.axis_size("tgt")
    column = lax.axis_index("tgt")
    src_lane = lax.axis_index("src")
    full_targets, full_sources = (
        lax.all_gather(target_rows, "src", axis=0, tiled=True),
        lax.all_gather(decoder_rows, "src", axis=0, tiled=True),
    )
    tgt_dev = full_targets.shape[0]
    src_dev = full_sources.shape[0]
    sub_rows = decoder_rows.shape[0]
    heads_here = out_proj.shape[0]
    head_dim = out_proj.shape[2]
    groups_here = value_proj.shape[0]
    repeat = heads_here // groups_here
    read_sum = jnp.einsum(
        "td,hde->the",
        full_targets,
        lax.all_gather(out_proj, "tgt", axis=1, tiled=True),
        preferred_element_type=jnp.float32,
    )
    head_reads = read_sum.astype(jnp.bfloat16).reshape(tgt_dev, groups_here, repeat, head_dim)
    values = jnp.einsum("sd,gde->sge", full_sources, value_proj, preferred_element_type=jnp.float32)
    values = values.astype(jnp.bfloat16).reshape(src_dev, groups_here * head_dim)
    attn_table = lax.all_gather(attention, "tgt", axis=1, tiled=True)
    target_attn = jnp.take(attn_table, target_pos, axis=1)
    keyed_attn = jnp.transpose(target_attn, (0, 2, 1))

    def edge_tile(payload, block_index):
        decoder_part, value_part = payload
        key_positions = lax.dynamic_slice_in_dim(source_pos, block_index * src_dev, src_dev)
        weights = jnp.take(keyed_attn, key_positions, axis=1).astype(jnp.float32)
        scores = jnp.einsum(
            "sgd,tgrd->grst",
            value_part.reshape(src_dev, groups_here, head_dim),
            head_reads,
            preferred_element_type=jnp.float32,
        )
        scores = scores.reshape(heads_here, src_dev, tgt_dev)
        mixed_term = jnp.sum(weights * scores, axis=0)
        own_positions = lax.dynamic_slice_in_dim(key_positions, src_lane * sub_rows, sub_rows)
        same_place = (own_positions[:, None] == target_pos[None, :]).astype(jnp.float32)
        direct = (
            jnp.einsum("sd,td->st", decoder_part, full_targets, preferred_element_type=jnp.float32)
            * same_place
        )
        own_rows = lax.dynamic_slice_in_dim(mixed_term, src_lane * sub_rows, sub_rows, 0)
        return lax.dynamic_update_slice_in_dim(
            mixed_term, own_rows + direct, src_lane * sub_rows, 0
        )

    def place_tile(partial_value, payload, block_index):
        kept_flag = tile_pattern[block_index, column]
        piece_tile = edge_tile(payload, block_index) * kept_flag.astype(jnp.float32)
        return lax.dynamic_update_slice_in_dim(partial_value, piece_tile, block_index * src_dev, 0)

    own_block = (decoder_rows, values)
    partial_value = jnp.zeros((blocks * src_dev, tgt_dev), jnp.float32)
    partial_value = place_tile(partial_value, own_block, column)

    def cycle_turn(turn_index, state_carry):
        forward_block, backward_block, running = state_carry
        forward_block = passed_along((forward_block[0], forward_block[1]), "tgt", 1)
        backward_block = passed_along((backward_block[0], backward_block[1]), "tgt", -1)
        running = place_tile(running, forward_block, (column - turn_index) % blocks)
        running = place_tile(running, backward_block, (column + turn_index) % blocks)
        return (forward_block, backward_block, running)

    forward_block, backward_block, partial_value = lax.fori_loop(
        1, blocks // 2, cycle_turn, (own_block, own_block, partial_value)
    )
    forward_block = passed_along((forward_block[0], forward_block[1]), "tgt", 1)
    partial_value = place_tile(partial_value, forward_block, (column - blocks // 2) % blocks)
    summed = lax.psum_scatter(partial_value, "src", scatter_dimension=0, tiled=True)
    return summed.astype(jnp.bfloat16)


def solution(mesh):
    return jax.shard_map(
        shards,
        mesh=mesh,
        in_specs=(
            P(("grp", "tgt", "src"), None),
            P(("grp", "tgt")),
            P(("grp", "tgt", "src"), None),
            P("grp"),
            P("src", "tgt", None),
            P("src", None, None),
            P(("grp", "src"), "tgt", None),
            P("grp", None),
        ),
        out_specs=P(("grp", "src"), "tgt"),
        check_vma=False,
    )
```

profile of v0, /device:TPU:0, one launch (start us, length us, event | category | flops | bytes accessed | tf_op | source)
XLA Modules:
  0.0 277.3 jit_solution(18094460157816442848)
XLA Ops:
  6.5 1.9 copy.26
  8.5 0.7 all-gather.6.cloned.1.call-update
  9.2 0.7 all-gather.8.cloned.1.call-update
  10.0 5.1 %collective-permute-start.3 = (bf16[16,4608]{1,0:T(8,128)(2,1)S(1)}, bf16[16,4608]{1,0:T(8,128)(2,1)S(1)}, u32[]{:S(2)}, u32[]{:S(2)}) collective-permute-start(bf16[16,4608]{1,0:T(8,128)(2,1)S(1)} %copy-done.2), channel_id=1, source_target_pairs={{0,12},{4,0},{8,4},{12,8},{1,13},{5,1},{9,5},{13,9},{2,14},{6,2},{... | collective-permute-start | bytes 442376 | tf_op jit(solution)/shard_map/while/body/eval_jaxpr/ppermute | solution.py:10
  15.1 7.5 %all_gather.15 = bf16[64,4608]{1,0:T(8,128)(2,1)S(1)} all-gather(bf16[16,4608]{1,0:T(8,128)(2,1)S(1)} %copy-done.2), channel_id=1, replica_groups=mesh['grp'=2,'tgt'=4,'src'=4] {'src'}, dimensions={0}, use_global_device_ids=true | all-gather | bytes 737280 | tf_op jit(solution)/shard_map/all_gather | solution.py:21
  22.6 3.3 %convolution_convert_fusion = bf16[64,4,128]{2,0,1:T(8,128)(2,1)S(1)} fusion(bf16[4,4608,128]{2,1,0:T(8,128)(2,1)} %param.15, bf16[64,4608]{1,0:T(8,128)(2,1)S(1)} %all_gather.15), kind=kOutput, calls=%fused_computation.8 | convolution fusion | flops 302022656 | bytes 5373952 | tf_op jit(solution)/shard_map/sd,gde->sge/dot_general | solution.py:37
  26.0 3.9 %collective-permute-start.2 = (bf16[64,512]{1,0:T(8,128)(2,1)S(1)}, bf16[64,512]{1,0:T(8,128)(2,1)S(1)}, u32[]{:S(2)}, u32[]{:S(2)}) collective-permute-start(bf16[64,512]{1,0:T(8,128)(2,1)S(1)} %copy_bitcast_fusion), channel_id=1, source_target_pairs={{0,12},{4,0},{8,4},{12,8},{1,13},{5,1},{9,5},{13,9},{2,14},{6,2},{... | collective-permute-start | bytes 196616 | tf_op jit(solution)/shard_map/while/body/eval_jaxpr/ppermute | solution.py:10
  30.1 0.7 fusion.26
  33.4 4.4 %collective-permute-done = bf16[64,512]{1,0:T(8,128)(2,1)S(1)} collective-permute-done((bf16[64,512]{1,0:T(8,128)(2,1)S(1)}, bf16[64,512]{1,0:T(8,128)(2,1)S(1)}, u32[]{:S(2)}, u32[]{:S(2)}) %collective-permute-start) | collective-permute-done | bytes 65568 | tf_op jit(solution)/shard_map/while/body/eval_jaxpr/ppermute | solution.py:10
  37.8 1.1 collective-permute-start.4
  39.0 5.8 %collective-permute-done.4 = bf16[64,512]{1,0:T(8,128)(2,1)S(1)} collective-permute-done((bf16[64,512]{1,0:T(8,128)(2,1)S(1)}, bf16[64,512]{1,0:T(8,128)(2,1)S(1)}, u32[]{:S(2)}, u32[]{:S(2)}) %collective-permute-start.4) | collective-permute-done | bytes 65568 | tf_op jit(solution)/shard_map/ppermute | solution.py:10
  44.9 2.0 gather_fusion
  46.9 0.9 select_bitcast_fusion
  47.8 1.3 copy.27
  49.1 0.6 gather_fusion.4
  49.7 0.6 gather_fusion.3
  50.3 0.6 gather_fusion.2
  50.9 0.6 gather_fusion.1
  51.5 17.4 %all-gather.6.cloned.1.call-done = bf16[256,4608]{1,0:T(8,128)(2,1)} async-done(((bf16[64,4608]{1,0:T(8,128)(2,1)}), bf16[256,4608]{1,0:T(8,128)(2,1)}) %all-gather.6.cloned.1.call-update) | async-done | bytes 2359312 | tf_op jit(solution)/shard_map/all_gather | solution.py:20
  68.9 168.4 %all-gather.8.cloned.1.call-done = bf16[8,4608,128]{2,1,0:T(8,128)(2,1)} async-done(((bf16[8,1152,128]{2,1,0:T(8,128)(2,1)}), bf16[8,4608,128]{2,1,0:T(8,128)(2,1)}) %all-gather.8.cloned.1.call-update) | async-done | bytes 9437200 | tf_op jit(solution)/shard_map/all_gather | solution.py:33
  237.2 7.0 %fusion.2 = bf16[256,8,128]{2,0,1:T(8,128)(2,1)S(1)} fusion(bf16[8,4608,128]{2,1,0:T(8,128)(2,1)} %all-gather.8.cloned.1.call-done, bf16[256,4608]{1,0:T(8,128)(2,1)} %all-gather.6.cloned.1.call-done), kind=kOutput, calls=%fused_computation.7 | convolution fusion | flops 2416181248 | bytes 12320768 | tf_op jit(solution)/shard_map/td,hde->the/dot_general | solution.py:30
  245.5 0.4 fusion.16
  245.9 0.4 fusion.17
  246.3 0.7 fusion.12
  247.1 0.7 fusion.10
  247.9 0.4 fusion.15
  248.3 0.7 fusion.8
  249.1 0.4 fusion.14
  249.5 0.7 fusion.6
  250.3 0.7 copy-done.1
  251.0 18.4 %reduce-scatter.2.cloned.1.call-done = f32[64,256]{1,0:T(8,128)} async-done(((f32[256,256]{1,0:T(8,128)}), f32[64,256]{1,0:T(8,128)}) %reduce-scatter.2.cloned.1.call-update) | async-done | bytes 65552 | tf_op jit(solution)/shard_map/reduce_scatter | solution.py:88
  269.3 1.5 convert_element_type.69
  (46 shorter events, 1.9 us)
Async XLA Ops:
  6.5 3.4 %copy-start.2 = (bf16[16,4608]{1,0:T(8,128)(2,1)S(1)}, bf16[16,4608]{1,0:T(8,128)(2,1)}, u32[]{:S(2)}) copy-start(bf16[16,4608]{1,0:T(8,128)(2,1)} %param.12) | copy-start | bytes 442372
  6.5 38.4 %all-gather.4.cloned.1.call-start = ((), (), s32[]{:S(2)}) async-start(), calls=%async_computation.1 | async-start | bytes 1310720 | tf_op jit(solution)/shard_map/all_gather | solution.py:39
  8.4 60.4 %all-gather.6.cloned.1.call-start = ((), (), s32[]{:S(2)}) async-start(), calls=%async_computation.2 | async-start | bytes 2949120 | tf_op jit(solution)/shard_map/all_gather | solution.py:20
  9.2 228.1 %all-gather.8.cloned.1.call-start = ((), (), s32[]{:S(2)}) async-start(), calls=%async_computation.3 | async-start | bytes 11796480 | tf_op jit(solution)/shard_map/all_gather | solution.py:33
  9.9 259.4 %reduce-scatter.2.cloned.1.call-start = ((), (), s32[]{:S(2)}) async-start(), calls=%async_computation.4 | async-start | bytes 327680 | tf_op jit(solution)/shard_map/reduce_scatter | solution.py:88
  10.0 238.3 %collective-permute-start.3 = (bf16[16,4608]{1,0:T(8,128)(2,1)S(1)}, bf16[16,4608]{1,0:T(8,128)(2,1)S(1)}, u32[]{:S(2)}, u32[]{:S(2)}) collective-permute-start(bf16[16,4608]{1,0:T(8,128)(2,1)S(1)} %copy-done.2), channel_id=1, source_target_pairs={{0,12},{4,0},{8,4},{12,8},{1,13},{5,1},{9,5},{13,9},{2,14},{6,2},{... | collective-permute-start | bytes 442376 | tf_op jit(solution)/shard_map/while/body/eval_jaxpr/ppermute | solution.py:10
  15.1 29.7 %collective-permute-start.1 = (bf16[16,4608]{1,0:T(8,128)(2,1)S(1)}, bf16[16,4608]{1,0:T(8,128)(2,1)S(1)}, u32[]{:S(2)}, u32[]{:S(2)}) collective-permute-start(bf16[16,4608]{1,0:T(8,128)(2,1)S(1)} %copy-done.2), channel_id=1, source_target_pairs={{0,4},{4,8},{8,12},{12,0},{1,5},{5,9},{9,13},{13,1},{2,6},{6,10},{... | collective-permute-start | bytes 442376 | tf_op jit(solution)/shard_map/while/body/eval_jaxpr/ppermute | solution.py:10
  22.6 7.2 %copy-start.3 = (s32[256]{0:T(256)S(1)}, s32[256]{0:T(256)}, u32[]{:S(2)}) copy-start(s32[256]{0:T(256)} %param.11) | copy-start | bytes 3076
  22.6 7.3 %copy-start.4 = (s32[256]{0:T(256)S(1)}, s32[256]{0:T(256)}, u32[]{:S(2)}) copy-start(s32[256]{0:T(256)} %param.13) | copy-start | bytes 3076
  22.6 7.5 %copy-start.5 = (s32[4,4]{1,0:T(4,128)S(1)}, s32[4,4]{1,0:T(4,128)}, u32[]{:S(2)}) copy-start(s32[4,4]{1,0:T(4,128)} %param.17) | copy-start | bytes 196
  26.0 13.0 %collective-permute-start.2 = (bf16[64,512]{1,0:T(8,128)(2,1)S(1)}, bf16[64,512]{1,0:T(8,128)(2,1)S(1)}, u32[]{:S(2)}, u32[]{:S(2)}) collective-permute-start(bf16[64,512]{1,0:T(8,128)(2,1)S(1)} %copy_bitcast_fusion), channel_id=1, source_target_pairs={{0,12},{4,0},{8,4},{12,8},{1,13},{5,1},{9,5},{13,9},{2,14},{6,2},{... | collective-permute-start | bytes 196616 | tf_op jit(solution)/shard_map/while/body/eval_jaxpr/ppermute | solution.py:10
  29.8 7.9 %collective-permute-start = (bf16[64,512]{1,0:T(8,128)(2,1)S(1)}, bf16[64,512]{1,0:T(8,128)(2,1)S(1)}, u32[]{:S(2)}, u32[]{:S(2)}) collective-permute-start(bf16[64,512]{1,0:T(8,128)(2,1)S(1)} %copy_bitcast_fusion), channel_id=1, source_target_pairs={{0,4},{4,8},{8,12},{12,0},{1,5},{5,9},{9,13},{13,1},{2,6},{6,10},{... | collective-permute-start | bytes 196616 | tf_op jit(solution)/shard_map/while/body/eval_jaxpr/ppermute | solution.py:10
  37.8 7.0 %collective-permute-start.4 = (bf16[64,512]{1,0:T(8,128)(2,1)S(1)}, bf16[64,512]{1,0:T(8,128)(2,1)S(1)}, u32[]{:S(2)}, u32[]{:S(2)}) collective-permute-start(bf16[64,512]{1,0:T(8,128)(2,1)S(1)} %collective-permute-done), channel_id=1, source_target_pairs={{0,4},{4,8},{8,12},{12,0},{1,5},{5,9},{9,13},{13,1},{2,6},{6,10},{... | collective-permute-start | bytes 196616 | tf_op jit(solution)/shard_map/ppermute | solution.py:10
  44.8 204.7 %collective-permute-start.5 = (bf16[16,4608]{1,0:T(8,128)(2,1)S(1)}, bf16[16,4608]{1,0:T(8,128)(2,1)S(1)}, u32[]{:S(2)}, u32[]{:S(2)}) collective-permute-start(bf16[16,4608]{1,0:T(8,128)(2,1)S(1)} %collective-permute-done.1), channel_id=1, source_target_pairs={{0,4},{4,8},{8,12},{12,0},{1,5},{5,9},{9,13},{13,1},{2,6},{6,10},{... | collective-permute-start | bytes 442376 | tf_op jit(solution)/shard_map/ppermute | solution.py:10
  244.5 1.8 copy-start
  250.3 0.7 copy-start.1
Sparse Core Ops, SparseCore 0:
  8.9 33.7 all-gather.3
  44.2 24.5 all-gather.5
  70.4 166.7 all-gather.7
  251.1 18.2 reduce-scatter.1
where the time goes:
time: 278 us; the launch traced here: 277 us
  waiting for transfers between devices  216 us (78%)
  between operations  16 us (6%)
  matrix products  14.3 us (5%)
  starting transfers between devices  10.4 us (4%)
  local copies, waits for them, and re-layouts  9.07 us (3%)
  blocking collectives  7.51 us (3%)
  other arithmetic  4.37 us (2%)
    all_gather x1, waiting for transfers between devices, shards(): lax.all_gather(out_proj, 'tgt', axis=1, tiled=True)  168 us
    reduce_scatter x1, waiting for transfers between devices, shards(): lax.psum_scatter(partial_value, 'src', scatter_dimension=0, tiled=True)  18.4 us
    all_gather x1, waiting for transfers between devices, shards(): lax.all_gather(target_rows, 'src', axis=0, tiled=True)  17.4 us
    ppermute x6, starting transfers between devices, passed_along(): return lax.ppermute(value, axis, pairs)  10.2 us
    ppermute x6, waiting for transfers between devices, passed_along(): return lax.ppermute(value, axis, pairs)  10.2 us
    all_gather x1, blocking collectives, shards(): lax.all_gather(decoder_rows, 'src', axis=0, tiled=True)  7.51 us
    dot_general x1, matrix products, shards(): jnp.einsum('td,hde->the', full_targets, lax.all_gather(out_proj, 'tgt', a...  6.99 us
  transfers between devices with their start and end apart: 10, of which 5 were waited for; matrix products, arithmetic and copies ran while one was open for 8% of the time, Pallas kernels for 0%

commit v1 on v0

--- a/solution.py
+++ b/solution.py
@@ -27,12 +27,26 @@
     head_dim = out_proj.shape[2]
     groups_here = value_proj.shape[0]
     repeat = heads_here // groups_here
+    length, index = (lax.axis_size("tgt"), lax.axis_index("tgt"))
+    backward = [(i, (i - 1) % length) for i in range(length)]
+    rows = out_proj.shape[1]
+    held = out_proj
     read_sum = jnp.einsum(
         "td,hde->the",
-        full_targets,
-        lax.all_gather(out_proj, "tgt", axis=1, tiled=True),
+        lax.dynamic_slice_in_dim(full_targets, index * rows, held.shape[1], axis=1),
+        held,
         preferred_element_type=jnp.float32,
     )
+    for step in range(1, length):
+        held = lax.ppermute(held, "tgt", backward)
+        read_sum = read_sum + jnp.einsum(
+            "td,hde->the",
+            lax.dynamic_slice_in_dim(
+                full_targets, (index + step) % length * rows, held.shape[1], axis=1
+            ),
+            held,
+            preferred_element_type=jnp.float32,
+        )
     head_reads = read_sum.astype(jnp.bfloat16).reshape(tgt_dev, groups_here, repeat, head_dim)
     values = jnp.einsum("sd,gde->sge", full_sources, value_proj, preferred_element_type=jnp.float32)
     values = values.astype(jnp.bfloat16).reshape(src_dev, groups_here * head_dim)

time: 278 us -> 257 us (0.924)
  waiting for transfers between devices: 216 us -> 169 us
  starting transfers between devices: 10.4 us -> 21.6 us
  local copies, waits for them, and re-layouts: 9.07 us -> 15 us
  matrix products: 14.3 us -> 19.8 us
  other arithmetic: 4.37 us -> 7.33 us
    all_gather x1 -> x0, waiting for transfers between devices: 168 us -> none  [shards(): lax.all_gather(out_proj, 'tgt', axis=1, tiled=True)]
    ppermute x0 -> x3, waiting for transfers between devices: none -> 100 us  [shards(): held = lax.ppermute(held, 'tgt', backward)]
    ppermute x6, waiting for transfers between devices: 10.2 us -> 49 us  [passed_along(): return lax.ppermute(value, axis, pairs)]
    all_gather x1, waiting for transfers between devices: 17.4 us -> 0.01 us  [shards(): lax.all_gather(target_rows, 'src', axis=0, tiled=True)]
    ppermute x0 -> x3, starting transfers between devices: none -> 13.6 us  [shards(): held = lax.ppermute(held, 'tgt', backward)]
    dot_general x4, matrix products: 2.81 us -> 6.47 us  [edge_tile(): jnp.einsum('sd,td->st', decoder_part, full_targets, preferred_element_typ...]
    gather x4, local copies, waits for them, and re-layouts: 2.38 us -> 5.46 us  [edge_tile(): weights = jnp.take(keyed_attn, key_positions, axis=1).astype(jnp.float32)]
    dot_general x1 -> x4, matrix products: 6.99 us -> 8.77 us  [the longest x3 5.94 us: shards(): jnp.einsum('td,hde->the', lax.dynamic_slice_in_dim(full_targets, (index +...]
  transfers between devices with their start and end apart: 10 -> 12, of which waited for: 5 -> 4; matrix products, arithmetic and copies ran while one was open for 8% -> 15% of each run, Pallas kernels for 0% -> 0%
where the time goes in v1:
time: 257 us
  waiting for transfers between devices  169 us (66%)
  starting transfers between devices  21.6 us (8%)
  matrix products  19.8 us (8%)
  between operations  16.1 us (6%)
  local copies, waits for them, and re-layouts  15 us (6%)
  blocking collectives  7.75 us (3%)
  other arithmetic  7.33 us (3%)
    ppermute x3, waiting for transfers between devices, shards(): held = lax.ppermute(held, 'tgt', backward)  100 us
    ppermute x6, waiting for transfers between devices, passed_along(): return lax.ppermute(value, axis, pairs)  49 us
    reduce_scatter x1, waiting for transfers between devices, shards(): lax.psum_scatter(partial_value, 'src', scatter_dimension=0, tiled=True)  19.9 us
    ppermute x3, starting transfers between devices, shards(): held = lax.ppermute(held, 'tgt', backward)  13.6 us
    ppermute x6, starting transfers between devices, passed_along(): return lax.ppermute(value, axis, pairs)  7.83 us
    all_gather x1, blocking collectives, shards(): lax.all_gather(decoder_rows, 'src', axis=0, tiled=True)  7.75 us
    dot_general x4, matrix products, edge_tile(): jnp.einsum('sd,td->st', decoder_part, full_targets, preferred_element_typ...  6.47 us
    dot_general x3, matrix products, shards(): jnp.einsum('td,hde->the', lax.dynamic_slice_in_dim(full_targets, (index +...  5.94 us
  transfers between devices with their start and end apart: 12, of which 4 were waited for; matrix products, arithmetic and copies ran while one was open for 15% of the time, Pallas kernels for 0%

profile of v1, /device:TPU:0, one launch (start us, length us, event | category | flops | bytes accessed | tf_op | source)
XLA Modules:
  0.0 256.8 jit_solution(4101901621774456490)
XLA Ops:
  6.5 5.1 %collective-permute-start = (bf16[8,1152,128]{2,1,0:T(8,128)(2,1)}, bf16[8,1152,128]{2,1,0:T(8,128)(2,1)S(1)}, u32[]{:S(2)}, u32[]{:S(2)}) collective-permute-start(bf16[8,1152,128]{2,1,0:T(8,128)(2,1)} %param.14), channel_id=1, source_target_pairs={{0,12},{4,0},{8,4},{12,8},{1,13},{5,1},{9,5},{13,9},{2,14},{6,2},{... | collective-permute-start | bytes 7077896 | tf_op jit(solution)/shard_map/ppermute | solution.py:41
  11.6 1.8 copy.26
  13.5 65.8 %collective-permute-done = bf16[8,1152,128]{2,1,0:T(8,128)(2,1)S(1)} collective-permute-done((bf16[8,1152,128]{2,1,0:T(8,128)(2,1)}, bf16[8,1152,128]{2,1,0:T(8,128)(2,1)S(1)}, u32[]{:S(2)}, u32[]{:S(2)}) %collective-permute-start) | collective-permute-done | bytes 2359328 | tf_op jit(solution)/shard_map/ppermute | solution.py:41
  79.3 4.2 %collective-permute-start.1 = (bf16[8,1152,128]{2,1,0:T(8,128)(2,1)S(1)}, bf16[8,1152,128]{2,1,0:T(8,128)(2,1)}, u32[]{:S(2)}, u32[]{:S(2)}) collective-permute-start(bf16[8,1152,128]{2,1,0:T(8,128)(2,1)S(1)} %collective-permute-done), channel_id=1, source_target_pairs={{0,12},{4,0},{8,4},{12,8},{1,13},{5,1},{9,5},{13,9},{2,14},{6,2},{... | collective-permute-start | bytes 7077896 | tf_op jit(solution)/shard_map/ppermute | solution.py:41
  83.6 7.7 %all_gather.11 = bf16[64,4608]{1,0:T(8,128)(2,1)S(1)} all-gather(bf16[16,4608]{1,0:T(8,128)(2,1)} %param.12), channel_id=1, replica_groups=mesh['grp'=2,'tgt'=4,'src'=4] {'src'}, dimensions={0}, use_global_device_ids=true | all-gather | bytes 737280 | tf_op jit(solution)/shard_map/all_gather | solution.py:21
  91.4 3.3 %convolution_convert_fusion = bf16[64,4,128]{2,0,1:T(8,128)(2,1)S(1)} fusion(bf16[4,4608,128]{2,1,0:T(8,128)(2,1)} %param.15, bf16[64,4608]{1,0:T(8,128)(2,1)S(1)} %all_gather.11), kind=kOutput, calls=%fused_computation.9 | convolution fusion | flops 302022656 | bytes 5373952 | tf_op jit(solution)/shard_map/sd,gde->sge/dot_general | solution.py:51
  94.8 3.9 %collective-permute-start.5 = (bf16[64,512]{1,0:T(8,128)(2,1)S(1)}, bf16[64,512]{1,0:T(8,128)(2,1)S(1)}, u32[]{:S(2)}, u32[]{:S(2)}) collective-permute-start(bf16[64,512]{1,0:T(8,128)(2,1)S(1)} %copy_bitcast_fusion), channel_id=1, source_target_pairs={{0,12},{4,0},{8,4},{12,8},{1,13},{5,1},{9,5},{13,9},{2,14},{6,2},{... | collective-permute-start | bytes 196616 | tf_op jit(solution)/shard_map/while/body/eval_jaxpr/ppermute | solution.py:10
  98.6 2.0 collective-permute-start.6
  100.6 34.5 %collective-permute-done.1 = bf16[8,1152,128]{2,1,0:T(8,128)(2,1)} collective-permute-done((bf16[8,1152,128]{2,1,0:T(8,128)(2,1)S(1)}, bf16[8,1152,128]{2,1,0:T(8,128)(2,1)}, u32[]{:S(2)}, u32[]{:S(2)}) %collective-permute-start.1) | collective-permute-done | bytes 2359328 | tf_op jit(solution)/shard_map/ppermute | solution.py:41
  135.1 4.4 %collective-permute-start.2 = (bf16[8,1152,128]{2,1,0:T(8,128)(2,1)}, bf16[8,1152,128]{2,1,0:T(8,128)(2,1)}, u32[]{:S(2)}, u32[]{:S(2)}) collective-permute-start(bf16[8,1152,128]{2,1,0:T(8,128)(2,1)} %collective-permute-done.1), channel_id=1, source_target_pairs={{0,12},{4,0},{8,4},{12,8},{1,13},{5,1},{9,5},{13,9},{2,14},{6,2},{... | collective-permute-start | bytes 7077896 | tf_op jit(solution)/shard_map/ppermute | solution.py:41
  139.5 0.7 compare_and_fusion
  144.7 0.7 fusion.36
  146.0 49.0 %collective-permute-done.7 = bf16[64,512]{1,0:T(8,128)(2,1)S(1)} collective-permute-done((bf16[64,512]{1,0:T(8,128)(2,1)S(1)}, bf16[64,512]{1,0:T(8,128)(2,1)S(1)}, u32[]{:S(2)}, u32[]{:S(2)}) %collective-permute-start.7) | collective-permute-done | bytes 65568 | tf_op jit(solution)/shard_map/ppermute | solution.py:10
  195.6 1.8 collective-permute-start.8
  197.5 2.0 gather_fusion
  199.5 2.2 select_bitcast_fusion
  201.7 2.2 copy.27
  203.9 1.4 gather_fusion.4
  205.3 1.4 gather_fusion.3
  206.7 1.3 gather_fusion.2
  208.1 1.3 gather_fusion.1
  209.4 2.8 %fusion.13 = f32[256,8,128]{2,0,1:T(8,128)S(1)} fusion(bf16[8,1152,128]{2,1,0:T(8,128)(2,1)} %param.14, bf16[256,4608]{1,0:T(8,128)(2,1)} %all-gather.5.cloned.1.call-done, s32[]{:T(128)S(6)} %select_n.126), kind=kOutput, calls=%fused_computation.27 | convolution fusion | flops 603979776 | bytes 3997700 | tf_op jit(solution)/shard_map/td,hde->the/dot_general | solution.py:34
  212.2 0.9 convolution_add_fusion.2
  213.1 2.5 convolution_add_fusion.1
  215.6 2.6 fusion
  220.4 1.6 fusion.8
  222.2 1.6 fusion.6
  224.3 1.6 fusion.4
  226.4 1.6 fusion.2
  228.1 0.7 copy-done.5
  228.8 19.9 %reduce-scatter.2.cloned.1.call-done = f32[64,256]{1,0:T(8,128)} async-done(((f32[256,256]{1,0:T(8,128)}), f32[64,256]{1,0:T(8,128)}) %reduce-scatter.2.cloned.1.call-update) | async-done | bytes 65552 | tf_op jit(solution)/shard_map/reduce_scatter | solution.py:102
  248.8 1.5 convert_element_type.69
  (78 shorter events, 6.6 us)
Async XLA Ops:
  6.5 190.9 %all-gather.3.cloned.1.call-start = ((), (), s32[]{:S(2)}) async-start(), calls=%async_computation.1 | async-start | bytes 1310720 | tf_op jit(solution)/shard_map/all_gather | solution.py:53
  6.5 72.8 %collective-permute-start = (bf16[8,1152,128]{2,1,0:T(8,128)(2,1)}, bf16[8,1152,128]{2,1,0:T(8,128)(2,1)S(1)}, u32[]{:S(2)}, u32[]{:S(2)}) collective-permute-start(bf16[8,1152,128]{2,1,0:T(8,128)(2,1)} %param.14), channel_id=1, source_target_pairs={{0,12},{4,0},{8,4},{12,8},{1,13},{5,1},{9,5},{13,9},{2,14},{6,2},{... | collective-permute-start | bytes 7077896 | tf_op jit(solution)/shard_map/ppermute | solution.py:41
  13.5 195.9 %all-gather.5.cloned.1.call-start = ((), (), s32[]{:S(2)}) async-start(), calls=%async_computation.2 | async-start | bytes 2949120 | tf_op jit(solution)/shard_map/all_gather | solution.py:20
  79.3 55.8 %collective-permute-start.1 = (bf16[8,1152,128]{2,1,0:T(8,128)(2,1)S(1)}, bf16[8,1152,128]{2,1,0:T(8,128)(2,1)}, u32[]{:S(2)}, u32[]{:S(2)}) collective-permute-start(bf16[8,1152,128]{2,1,0:T(8,128)(2,1)S(1)} %collective-permute-done), channel_id=1, source_target_pairs={{0,12},{4,0},{8,4},{12,8},{1,13},{5,1},{9,5},{13,9},{2,14},{6,2},{... | collective-permute-start | bytes 7077896 | tf_op jit(solution)/shard_map/ppermute | solution.py:41
  83.5 165.3 %reduce-scatter.2.cloned.1.call-start = ((), (), s32[]{:S(2)}) async-start(), calls=%async_computation.3 | async-start | bytes 327680 | tf_op jit(solution)/shard_map/reduce_scatter | solution.py:102
  83.5 112.1 %collective-permute-start.4 = (bf16[16,4608]{1,0:T(8,128)(2,1)}, bf16[16,4608]{1,0:T(8,128)(2,1)}, u32[]{:S(2)}, u32[]{:S(2)}) collective-permute-start(bf16[16,4608]{1,0:T(8,128)(2,1)} %param.12), channel_id=1, source_target_pairs={{0,4},{4,8},{8,12},{12,0},{1,5},{5,9},{9,13},{13,1},{2,6},{6,10},{... | collective-permute-start | bytes 442376 | tf_op jit(solution)/shard_map/while/body/eval_jaxpr/ppermute | solution.py:10
  91.4 48.1 %copy-start.8 = (s32[256]{0:T(256)S(1)}, s32[256]{0:T(256)}, u32[]{:S(2)}) copy-start(s32[256]{0:T(256)} %param.11) | copy-start | bytes 3076
  91.4 48.2 %copy-start.9 = (s32[256]{0:T(256)S(1)}, s32[256]{0:T(256)}, u32[]{:S(2)}) copy-start(s32[256]{0:T(256)} %param.13) | copy-start | bytes 3076
  91.4 50.0 %copy-start.14 = (s32[4,4]{1,0:T(4,128)S(1)}, s32[4,4]{1,0:T(4,128)}, u32[]{:S(2)}) copy-start(s32[4,4]{1,0:T(4,128)} %param.17) | copy-start | bytes 196
  94.7 49.9 %collective-permute-start.3 = (bf16[64,512]{1,0:T(8,128)(2,1)S(1)}, bf16[64,512]{1,0:T(8,128)(2,1)S(1)}, u32[]{:S(2)}, u32[]{:S(2)}) collective-permute-start(bf16[64,512]{1,0:T(8,128)(2,1)S(1)} %copy_bitcast_fusion), channel_id=1, source_target_pairs={{0,4},{4,8},{8,12},{12,0},{1,5},{5,9},{9,13},{13,1},{2,6},{6,10},{... | collective-permute-start | bytes 196616 | tf_op jit(solution)/shard_map/while/body/eval_jaxpr/ppermute | solution.py:10
  94.8 50.6 %collective-permute-start.5 = (bf16[64,512]{1,0:T(8,128)(2,1)S(1)}, bf16[64,512]{1,0:T(8,128)(2,1)S(1)}, u32[]{:S(2)}, u32[]{:S(2)}) collective-permute-start(bf16[64,512]{1,0:T(8,128)(2,1)S(1)} %copy_bitcast_fusion), channel_id=1, source_target_pairs={{0,12},{4,0},{8,4},{12,8},{1,13},{5,1},{9,5},{13,9},{2,14},{6,2},{... | collective-permute-start | bytes 196616 | tf_op jit(solution)/shard_map/while/body/eval_jaxpr/ppermute | solution.py:10
  98.6 125.7 %collective-permute-start.6 = (bf16[16,4608]{1,0:T(8,128)(2,1)}, bf16[16,4608]{1,0:T(8,128)(2,1)}, u32[]{:S(2)}, u32[]{:S(2)}) collective-permute-start(bf16[16,4608]{1,0:T(8,128)(2,1)} %param.12), channel_id=1, source_target_pairs={{0,12},{4,0},{8,4},{12,8},{1,13},{5,1},{9,5},{13,9},{2,14},{6,2},{... | collective-permute-start | bytes 442376 | tf_op jit(solution)/shard_map/while/body/eval_jaxpr/ppermute | solution.py:10
  135.1 80.5 %collective-permute-start.2 = (bf16[8,1152,128]{2,1,0:T(8,128)(2,1)}, bf16[8,1152,128]{2,1,0:T(8,128)(2,1)}, u32[]{:S(2)}, u32[]{:S(2)}) collective-permute-start(bf16[8,1152,128]{2,1,0:T(8,128)(2,1)} %collective-permute-done.1), channel_id=1, source_target_pairs={{0,12},{4,0},{8,4},{12,8},{1,13},{5,1},{9,5},{13,9},{2,14},{6,2},{... | collective-permute-start | bytes 7077896 | tf_op jit(solution)/shard_map/ppermute | solution.py:41
  144.6 50.4 %collective-permute-start.7 = (bf16[64,512]{1,0:T(8,128)(2,1)S(1)}, bf16[64,512]{1,0:T(8,128)(2,1)S(1)}, u32[]{:S(2)}, u32[]{:S(2)}) collective-permute-start(bf16[64,512]{1,0:T(8,128)(2,1)S(1)} %collective-permute-done.3), channel_id=1, source_target_pairs={{0,4},{4,8},{8,12},{12,0},{1,5},{5,9},{9,13},{13,1},{2,6},{6,10},{... | collective-permute-start | bytes 196616 | tf_op jit(solution)/shard_map/ppermute | solution.py:10
  195.6 30.8 %collective-permute-start.8 = (bf16[16,4608]{1,0:T(8,128)(2,1)}, bf16[16,4608]{1,0:T(8,128)(2,1)}, u32[]{:S(2)}, u32[]{:S(2)}) collective-permute-start(bf16[16,4608]{1,0:T(8,128)(2,1)} %collective-permute-done.4), channel_id=1, source_target_pairs={{0,4},{4,8},{8,12},{12,0},{1,5},{5,9},{9,13},{13,1},{2,6},{6,10},{... | collective-permute-start | bytes 442376 | tf_op jit(solution)/shard_map/ppermute | solution.py:10
  209.3 2.8 %copy-start = (bf16[256,4608]{1,0:T(8,128)(2,1)S(1)}, bf16[256,4608]{1,0:T(8,128)(2,1)}, u32[]{:S(2)}) copy-start(bf16[256,4608]{1,0:T(8,128)(2,1)} %all-gather.5.cloned.1.call-done) | copy-start | bytes 7077892
  215.6 2.9 %copy-start.7 = (bf16[64,4,128]{2,1,0:T(4,128)(2,1)S(1)}, bf16[64,4,128]{2,1,0:T(4,128)(2,1)}, u32[]{:S(2)}) copy-start(bf16[64,4,128]{2,1,0:T(4,128)(2,1)} %reshape.57) | copy-start | bytes 196612
  215.6 3.3 %copy-start.6 = (bf16[64,4,128]{2,1,0:T(4,128)(2,1)S(1)}, bf16[64,4,128]{2,1,0:T(4,128)(2,1)}, u32[]{:S(2)}) copy-start(bf16[64,4,128]{2,1,0:T(4,128)(2,1)} %reshape.55) | copy-start | bytes 196612
  218.2 1.3 copy-start.4
  218.2 1.3 copy-start.13
  218.5 1.4 copy-start.3
  218.5 1.4 copy-start.12
  218.5 1.9 copy-start.18
  219.5 2.7 %copy-start.17 = (s32[16]{0:T(128)S(1)}, s32[16]{0:T(128)}, u32[]{:S(2)}) copy-start(s32[16]{0:T(128)} %get-tuple-element.65) | copy-start | bytes 196
  220.4 3.4 %copy-start.2 = (bf16[64,8,256]{2,1,0:T(8,128)(2,1)S(1)}, bf16[64,8,256]{2,1,0:T(8,128)(2,1)}, u32[]{:S(2)}) copy-start(bf16[64,8,256]{2,1,0:T(8,128)(2,1)} %gather_fusion.3) | copy-start | bytes 786436
  220.4 3.4 %copy-start.11 = (pred[64]{0:T(512)(128)(4,1)S(1)}, pred[64]{0:T(512)(128)(4,1)}, u32[]{:S(2)}) copy-start(pred[64]{0:T(512)(128)(4,1)} %get-tuple-element.67) | copy-start | bytes 196
  222.1 2.2 copy-start.16
  223.8 2.2 copy-start.1
  223.8 2.2 copy-start.10
  223.8 2.6 %copy-start.15 = (s32[16]{0:T(128)S(1)}, s32[16]{0:T(128)}, u32[]{:S(2)}) copy-start(s32[16]{0:T(128)} %get-tuple-element.62) | copy-start | bytes 196
  228.1 0.7 copy-start.5
Sparse Core Ops, SparseCore 0:
  13.6 40.0 all-gather.2
  83.6 23.4 all-gather.4
  228.9 19.7 reduce-scatter.1
